TPU v7x, 32 devices: a whole 2x2x4 slice. The times are simulated.
32 devices in a mesh: grp: 4 (over y, x), dev: 8 (over z, core).
Axes of the slice: x: 2, y: 2, z: 4, core: 2. Of those that a mesh axis runs over, the one named last changes fastest.
Arguments:
- table: float32 [262144, 128], P(('grp', 'dev')), may hold values from -6 to 6
- cold_grads: float32 [131072, 128], P(('grp', 'dev')), may hold values from -6 to 6
- cold_owner: int32 [131072, 1], P(('grp', 'dev')), may hold values from 0 to 31; in each aligned block of 4096 rows (0 to 4095, 4096 to 8191, ...) at most 256 rows name the same one
- cold_row: int32 [131072], P(('grp', 'dev')), may hold values from 0 to 8191
- hot_grads: float32 [32768, 128], P(('grp', 'dev')), may hold values from -6 to 6
- hot_slot: int32 [32768], P(('grp', 'dev')), may hold values from 0 to 255
- hot_ids: int32 [256], replicated, may hold values from 0 to 262143, as said below
Outputs:
- new_table: float32 [262144, 128], P(('grp', 'dev'))
Inputs may be any that keep to these rules, and one draw needn't show every extreme that they name: `cold_owner`: among the 4096 rare-row lookups of one device no owner is named more than 256 times, a bound that some block reaches. `hot_ids`: all entries differ.
All inputs are finite; a program needn't handle non-finite values.
Results may differ from a plain program's by a relative error of at most 0.00005.
Values sent between devices are 32-bit elements; how exact they have to be, the bound alone decides.
A program may use at most 64 MiB of HBM per device.

v0:
```python
import jax
import jax.numpy as jnp
from jax import lax
from jax.sharding import PartitionSpec as P

LEARN = 0.05


def hot_update(table, hot_grads, hot_slot, hot_ids):
    count = hot_ids.shape[0]
    pick = (jnp.arange(count, dtype=jnp.int32)[:, None] == hot_slot[None, :]).astype(jnp.float32)
    partial_sum = jnp.dot(
        pick, hot_grads, precision=lax.Precision.HIGHEST, preferred_element_type=jnp.float32
    )
    share = lax.psum_scatter(partial_sum, "dev", scatter_dimension=0, tiled=True)
    share = lax.psum(share, "grp")
    total = lax.all_gather(share, "dev", axis=0, tiled=True)
    rows_dev = table.shape[0]
    local = hot_ids - lax.axis_index(("grp", "dev")) * rows_dev
    inside = (local >= 0) & (local < rows_dev)
    target = jnp.where(inside, local, rows_dev)
    return table.at[target].add(-LEARN * total, mode="drop")


def pack_cold(cold_grads, cold_owner, cold_row, devices, slots):
    owner = cold_owner[:, 0]
    onehot = (owner[:, None] == jnp.arange(devices, dtype=jnp.int32)[None, :]).astype(jnp.int32)
    running = jnp.cumsum(onehot, axis=0) - 1
    rank = jnp.sum(running * onehot, axis=1)
    target = owner * slots + rank
    width = cold_grads.shape[1]
    send_grads = jnp.zeros((devices * slots, width), jnp.float32).at[target].set(cold_grads)
    send_rows = jnp.zeros((devices * slots,), jnp.int32).at[target].set(cold_row)
    return (send_grads, send_rows)


def on_device(table, cold_grads, cold_owner, cold_row, hot_grads, hot_slot, hot_ids):
    n_grp = lax.axis_size("grp")
    n_dev = lax.axis_size("dev")
    devices = n_grp * n_dev
    width = table.shape[1]
    slots = max(4, 2 * cold_grads.shape[0] // devices)
    send_grads, send_rows = pack_cold(cold_grads, cold_owner, cold_row, devices, slots)
    grads_four = send_grads.reshape(n_grp, n_dev, slots, width)
    rows_three = send_rows.reshape(n_grp, n_dev, slots)
    got_grads, got_rows = (
        lax.all_to_all(
            lax.all_to_all(grads_four, "grp", split_axis=0, concat_axis=0, tiled=True),
            "dev",
            split_axis=1,
            concat_axis=1,
            tiled=True,
        ),
        lax.all_to_all(
            lax.all_to_all(rows_three, "grp", split_axis=0, concat_axis=0, tiled=True),
            "dev",
            split_axis=1,
            concat_axis=1,
            tiled=True,
        ),
    )
    current = hot_update(table, hot_grads, hot_slot, hot_ids)
    current = current.at[got_rows.reshape(-1)].add(-LEARN * got_grads.reshape(-1, width))
    return current


def solution(mesh):
    in_specs = (
        P(("grp", "dev"), None),
        P(("grp", "dev"), None),
        P(("grp", "dev"), None),
        P(("grp", "dev")),
        P(("grp", "dev"), None),
        P(("grp", "dev")),
        P(),
    )
    out_specs = P(("grp", "dev"), None)
    return jax.shard_map(
        on_device, mesh=mesh, in_specs=in_specs, out_specs=out_specs, check_vma=False
    )
```

profile of v0, /device:TPU:4, one launch (start us, length us, event | category | flops | bytes accessed | tf_op | source)
XLA Modules:
  0.0 298.4 jit_solution(3252168921994145079)
XLA Ops:
  6.5 4.5 %copy.23 = f32[8192,128]{1,0:T(8,128)} copy(f32[8192,128]{1,0:T(8,128)} %param.7) | data formatting | bytes 8388608
  11.1 9.2 %reduce-window.6 = s32[32,32,128]{2,1,0:T(8,128)S(1)} reduce-window(s32[32,32,128]{2,1,0:T(8,128)S(1)} %fusion.6, s32[]{:T(128)} %constant.13.clone.1), window={size=1x1x128 pad=0_0x0_0x127_0}, to_apply=%region_3.4 | reduce-window | flops 16646144 | bytes 1048580 | tf_op jit(solution)/shard_map/reduce-window
  20.4 0.8 slice_reduce_fusion
  21.2 0.2 reduce-window.9
  21.4 0.2 add_add_fusion
  21.6 0.3 fusion.4
  21.9 15.7 %scatter_custom_fusion.1 = s32[8192]{0:T(1024)S(1)} fusion(s32[4096]{0:T(1024)S(1)} %bitcast.30, s32[4096]{0:T(1024)} %param.10, s32[]{:T(128)} %constant.13.clone.1), kind=kCustom, calls=%fused_computation.23 | custom fusion | bytes 33280 | tf_op jit(solution)/shard_map/scatter | solution.py:33
  37.7 0.6 reshape.61
  38.3 4.2 %all-to-all-start = ((s32[4,8,256]{2,1,0:T(8,128)}), s32[4,8,256]{2,1,0:T(8,128)S(1)}, u32[]{:S(2)}, u32[]{:S(2)}) async-start(s32[4,8,256]{2,1,0:T(8,128)} %reshape.61), calls=%async_computation.1 | async-start | bytes 65536 | tf_op jit(solution)/shard_map/all_to_all | solution.py:55
  42.5 13.1 %scatter_custom_fusion.2 = f32[8192,128]{1,0:T(8,128)} fusion(s32[4096]{0:T(1024)S(1)} %bitcast.31, f32[4096,128]{1,0:T(8,128)} %param.8, f32[]{:T(128)} %constant.17.clone.1), kind=kCustom, calls=%fused_computation.5 | custom fusion | bytes 4194816 | tf_op jit(solution)/shard_map/scatter | solution.py:32
  55.6 4.9 %all-to-all-start.2 = ((f32[4,8,256,128]{3,2,1,0:T(8,128)}), f32[4,8,256,128]{3,2,1,0:T(8,128)}, u32[]{:S(2)}, u32[]{:S(2)}) async-start(f32[4,8,256,128]{3,2,1,0:T(8,128)} %bitcast.23), calls=%async_computation.3 | async-start | bytes 8388608 | tf_op jit(solution)/shard_map/all_to_all | solution.py:48
  60.4 0.6 copy.13
  61.0 46.2 %all-to-all-done.2 = f32[4,8,256,128]{3,2,1,0:T(8,128)} async-done(((f32[4,8,256,128]{3,2,1,0:T(8,128)}), f32[4,8,256,128]{3,2,1,0:T(8,128)}, u32[]{:S(2)}, u32[]{:S(2)}) %all-to-all-start.2) | async-done | bytes 4194336 | tf_op jit(solution)/shard_map/all_to_all | solution.py:48
  107.3 4.9 %all-to-all-start.1 = ((s32[4,8,256]{2,0,1:T(4,128)}), s32[4,8,256]{2,0,1:T(4,128)S(1)}, u32[]{:S(2)}, u32[]{:S(2)}) async-start(s32[4,8,256]{2,0,1:T(4,128)} %copy.13), calls=%async_computation.2 | async-start | bytes 65536 | tf_op jit(solution)/shard_map/all_to_all | solution.py:54
  112.1 4.6 %copy.15 = f32[4,8,256,128]{3,2,0,1:T(8,128)} copy(f32[4,8,256,128]{3,2,1,0:T(8,128)} %all-to-all-done.2) | data formatting | bytes 8388608 | tf_op jit(solution)/shard_map/all_to_all | solution.py:48
  116.7 1.2 all-to-all-done.1
  117.9 4.5 %all-to-all-start.3 = ((f32[4,8,256,128]{3,2,0,1:T(8,128)}), f32[4,8,256,128]{3,2,0,1:T(8,128)}, u32[]{:S(2)}, u32[]{:S(2)}) async-start(f32[4,8,256,128]{3,2,0,1:T(8,128)} %copy.15), calls=%async_computation.4 | async-start | bytes 8388608 | tf_op jit(solution)/shard_map/all_to_all | solution.py:47
  122.5 1.3 fusion.2
  124.0 33.3 %reduce-scatter.2.cloned.1.call-done = f32[32,128]{1,0:T(8,128)} async-done(((f32[256,128]{1,0:T(8,128)}), f32[32,128]{1,0:T(8,128)}) %reduce-scatter.2.cloned.1.call-update) | async-done | bytes 16400 | tf_op jit(solution)/shard_map/reduce_scatter | solution.py:15
  157.3 15.7 %psum.7 = f32[32,128]{1,0:T(8,128)S(1)} all-reduce(f32[32,128]{1,0:T(8,128)} %reduce-scatter.2.cloned.1.call-done), channel_id=1, replica_groups=mesh['grp'=4,'dev'=8] {'grp'}, use_global_device_ids=true, to_apply=%region_1.2 | all-reduce | flops 4096 | bytes 32768 | tf_op jit(solution)/shard_map/psum | solution.py:16
  172.9 50.9 %all_gather.3 = f32[256,128]{1,0:T(8,128)S(1)} all-gather(f32[32,128]{1,0:T(8,128)S(1)} %psum.7), channel_id=1, replica_groups=mesh['grp'=4,'dev'=8] {'dev'}, dimensions={0}, use_global_device_ids=true | all-gather | bytes 147456 | tf_op jit(solution)/shard_map/all_gather | solution.py:17
  223.9 6.0 %scatter_custom_fusion = f32[8192,128]{1,0:T(8,128)} fusion(f32[8192,128]{1,0:T(8,128)} %copy.23, s32[256]{0:T(256)S(1)} %compare_select_fusion.2, f32[256,128]{1,0:T(8,128)S(1)} %all_gather.3, f32[]{:T(128)} %constant.14.clone.1), kind=kCustom, calls=%fused_computation.19 | custom fusion | flops 65536 | bytes 4325888 | tf_op jit(solution)/shard_map/scatter-add | solution.py:22
  229.9 4.7 %copy_multiply_fusion = f32[4,8,256,128]{3,2,1,0:T(8,128)} fusion(f32[4,8,256,128]{3,2,0,1:T(8,128)} %all-to-all-done.3), kind=kLoop, calls=%fused_computation.4 | loop fusion | flops 1048576 | bytes 8388608 | tf_op jit(solution)/shard_map/mul | solution.py:63
  234.6 57.0 %scatter_fusion = f32[8192,128]{1,0:T(8,128)} fusion(f32[8192,128]{1,0:T(8,128)} %scatter_custom_fusion, s32[8192]{0:T(1024)S(1)} %bitcast.27, f32[8192,128]{1,0:T(8,128)} %bitcast.22), kind=kCustom, calls=%fused_computation.3 | custom fusion | flops 1048576 | bytes 12615680 | tf_op jit(solution)/shard_map/scatter-add | solution.py:63
  (18 shorter events, 0.2 us)
Async XLA Ops:
  6.5 116.0 %copy-start = (f32[1024,128]{1,0:T(8,128)S(1)}, f32[1024,128]{1,0:T(8,128)}, u32[]{:S(2)}) copy-start(f32[1024,128]{1,0:T(8,128)} %param.11) | copy-start | bytes 1572868
  6.5 4.5 %copy-start.1 = (s32[4096,1]{0,1:T(1,128)S(1)}, s32[4096,1]{0,1:T(1,128)}, u32[]{:S(2)}) copy-start(s32[4096,1]{0,1:T(1,128)} %param.9) | copy-start | bytes 49156
  38.3 17.3 %all-to-all-start = ((s32[4,8,256]{2,1,0:T(8,128)}), s32[4,8,256]{2,1,0:T(8,128)S(1)}, u32[]{:S(2)}, u32[]{:S(2)}) async-start(s32[4,8,256]{2,1,0:T(8,128)} %reshape.61), calls=%async_computation.1 | async-start | bytes 65536 | tf_op jit(solution)/shard_map/all_to_all | solution.py:55
  55.6 51.7 %all-to-all-start.2 = ((f32[4,8,256,128]{3,2,1,0:T(8,128)}), f32[4,8,256,128]{3,2,1,0:T(8,128)}, u32[]{:S(2)}, u32[]{:S(2)}) async-start(f32[4,8,256,128]{3,2,1,0:T(8,128)} %bitcast.23), calls=%async_computation.3 | async-start | bytes 8388608 | tf_op jit(solution)/shard_map/all_to_all | solution.py:48
  107.3 10.6 %all-to-all-start.1 = ((s32[4,8,256]{2,0,1:T(4,128)}), s32[4,8,256]{2,0,1:T(4,128)S(1)}, u32[]{:S(2)}, u32[]{:S(2)}) async-start(s32[4,8,256]{2,0,1:T(4,128)} %copy.13), calls=%async_computation.2 | async-start | bytes 65536 | tf_op jit(solution)/shard_map/all_to_all | solution.py:54
  116.7 5.8 %copy-start.2 = (s32[1024]{0:T(1024)S(1)}, s32[1024]{0:T(1024)}, u32[]{:S(2)}) copy-start(s32[1024]{0:T(1024)} %param.12) | copy-start | bytes 12292
  116.7 7.2 %copy-start.3 = (s32[256]{0:T(256)S(1)}, s32[256]{0:T(256)}, u32[]{:S(2)}) copy-start(s32[256]{0:T(256)} %param.13) | copy-start | bytes 3076
  117.9 112.0 %all-to-all-start.3 = ((f32[4,8,256,128]{3,2,0,1:T(8,128)}), f32[4,8,256,128]{3,2,0,1:T(8,128)}, u32[]{:S(2)}, u32[]{:S(2)}) async-start(f32[4,8,256,128]{3,2,0,1:T(8,128)} %copy.15), calls=%async_computation.4 | async-start | bytes 8388608 | tf_op jit(solution)/shard_map/all_to_all | solution.py:47
  122.4 34.8 %reduce-scatter.2.cloned.1.call-start = ((), (), s32[]{:S(2)}) async-start(), calls=%async_computation.5 | async-start | bytes 147456 | tf_op jit(solution)/shard_map/reduce_scatter | solution.py:15
Sparse Core Ops, SparseCore 0:
  125.5 31.7 reduce-scatter.1
where the time goes:
time: 299 us; the launch traced here: 298 us
  waiting for transfers between devices  80.7 us (27%)
  other arithmetic  77.8 us (26%)
  blocking collectives  66.6 us (22%)
  local copies, waits for them, and re-layouts  39.9 us (13%)
  starting transfers between devices  18.6 us (6%)
  between operations  13.5 us (5%)
    scatter-add x1, other arithmetic, on_device(): current.at[got_rows.reshape(-1)].add(-LEARN * got_grads.reshape(-1, width))  57 us
    all_gather x1, blocking collectives, hot_update(): total = lax.all_gather(share, 'dev', axis=0, tiled=True)  50.9 us
    all_to_all x1, waiting for transfers between devices, on_device(): lax.all_to_all(grads_four, 'grp', split_axis=0, concat_axis=0, tiled=True)  46.2 us
    reduce_scatter x1, waiting for transfers between devices, hot_update(): lax.psum_scatter(partial_sum, 'dev', scatter_dimension=0, tiled=True)  33.3 us
    scatter x1, local copies, waits for them, and re-layouts, pack_cold(): jnp.zeros((devices * slots,), jnp.int32).at[target].set(cold_row)  15.7 us
    psum x1, blocking collectives, hot_update(): share = lax.psum(share, 'grp')  15.7 us
    scatter x1, local copies, waits for them, and re-layouts, pack_cold(): jnp.zeros((devices * slots, width), jnp.float32).at[target].set(cold_grads)  13.1 us
    another operation x2, other arithmetic  9.41 us
  transfers between devices with their start and end apart: 5, of which 3 were waited for; matrix products, arithmetic and copies ran while one was open for 9% of the time, Pallas kernels for 0%

commit v1 on v0

--- a/solution.py
+++ b/solution.py
@@ -4,6 +4,13 @@
 from jax.sharding import PartitionSpec as P
 
 LEARN = 0.05
+
+
+def stacked_exchange(x, mesh_axis, split, join):
+    size = lax.axis_size(mesh_axis)
+    pieces = jnp.stack(jnp.split(x, size, axis=split), axis=0)
+    pieces = lax.all_to_all(pieces, mesh_axis, split_axis=0, concat_axis=0)
+    return jnp.concatenate(pieces, axis=join)
 
 
 def hot_update(table, hot_grads, hot_slot, hot_ids):
@@ -44,12 +51,8 @@
     grads_four = send_grads.reshape(n_grp, n_dev, slots, width)
     rows_three = send_rows.reshape(n_grp, n_dev, slots)
     got_grads, got_rows = (
-        lax.all_to_all(
-            lax.all_to_all(grads_four, "grp", split_axis=0, concat_axis=0, tiled=True),
-            "dev",
-            split_axis=1,
-            concat_axis=1,
-            tiled=True,
+        stacked_exchange(
+            lax.all_to_all(grads_four, "grp", split_axis=0, concat_axis=0, tiled=True), "dev", 1, 1
         ),
         lax.all_to_all(
             lax.all_to_all(rows_three, "grp", split_axis=0, concat_axis=0, tiled=True),

time: 299 us -> 310 us (1.037)
  local copies, waits for them, and re-layouts: 39.9 us -> 52.7 us
    unnamed x9 -> x16, local copies, waits for them, and re-layouts: 4.56 us -> 17.7 us
    all_to_all x1 -> x0, local copies, waits for them, and re-layouts: 4.57 us -> none  [on_device(): lax.all_to_all(grads_four, 'grp', split_axis=0, concat_axis=0, tiled=True)]
  transfers between devices with their start and end apart: 5 -> 5, of which waited for: 3 -> 2; matrix products, arithmetic and copies ran while one was open for 9% -> 12% of each run, Pallas kernels for 0% -> 0%
where the time goes in v1:
time: 310 us; the launch traced here: 309 us
  waiting for transfers between devices  79.6 us (26%)
  other arithmetic  75.6 us (24%)
  blocking collectives  66.7 us (22%)
  local copies, waits for them, and re-layouts  52.7 us (17%)
  starting transfers between devices  19.2 us (6%)
  between operations  13.5 us (4%)
    scatter-add x1, other arithmetic, on_device(): current.at[got_rows.reshape(-1)].add(-LEARN * got_grads.reshape(-1, width))  57 us
    all_gather x1, blocking collectives, hot_update(): total = lax.all_gather(share, 'dev', axis=0, tiled=True)  51 us
    all_to_all x1, waiting for transfers between devices, on_device(): lax.all_to_all(grads_four, 'grp', split_axis=0, concat_axis=0, tiled=True)  46.2 us
    reduce_scatter x1, waiting for transfers between devices, hot_update(): lax.psum_scatter(partial_sum, 'dev', scatter_dimension=0, tiled=True)  33.3 us
    unnamed x16, local copies, waits for them, and re-layouts  17.7 us
    scatter x1, local copies, waits for them, and re-layouts, pack_cold(): jnp.zeros((devices * slots,), jnp.int32).at[target].set(cold_row)  15.7 us
    psum x1, blocking collectives, hot_update(): share = lax.psum(share, 'grp')  15.7 us
    scatter x1, local copies, waits for them, and re-layouts, pack_cold(): jnp.zeros((devices * slots, width), jnp.float32).at[target].set(cold_grads)  13.1 us
  transfers between devices with their start and end apart: 5, of which 2 were waited for; matrix products, arithmetic and copies ran while one was open for 12% of the time, Pallas kernels for 0%

profile of v1, /device:TPU:4, one launch (start us, length us, event | category | flops | bytes accessed | tf_op | source)
XLA Modules:
  0.0 308.7 jit_solution(2356779726733863759)
XLA Ops:
  6.5 4.5 %copy.67 = f32[8192,128]{1,0:T(8,128)} copy(f32[8192,128]{1,0:T(8,128)} %param.7) | data formatting | bytes 8388608
  11.1 9.2 %reduce-window.6 = s32[32,32,128]{2,1,0:T(8,128)S(1)} reduce-window(s32[32,32,128]{2,1,0:T(8,128)S(1)} %fusion.14, s32[]{:T(128)} %constant.13.clone.1), window={size=1x1x128 pad=0_0x0_0x127_0}, to_apply=%region_3.4 | reduce-window | flops 16646144 | bytes 1048580 | tf_op jit(solution)/shard_map/reduce-window
  21.9 15.7 %scatter_custom_fusion.1 = s32[8192]{0:T(1024)S(1)} fusion(s32[4096]{0:T(1024)S(1)} %bitcast.80, s32[4096]{0:T(1024)} %param.10, s32[]{:T(128)} %constant.13.clone.1), kind=kCustom, calls=%fused_computation.39 | custom fusion | bytes 33280 | tf_op jit(solution)/shard_map/scatter | solution.py:40
  38.3 4.2 %all-to-all-start = ((s32[4,8,256]{2,1,0:T(8,128)}), s32[4,8,256]{2,1,0:T(8,128)S(1)}, u32[]{:S(2)}, u32[]{:S(2)}) async-start(s32[4,8,256]{2,1,0:T(8,128)} %reshape.61), calls=%async_computation.1 | async-start | bytes 65536 | tf_op jit(solution)/shard_map/all_to_all | solution.py:58
  42.5 13.1 %scatter_custom_fusion.2 = f32[8192,128]{1,0:T(8,128)} fusion(s32[4096]{0:T(1024)S(1)} %bitcast.81, f32[4096,128]{1,0:T(8,128)} %param.8, f32[]{:T(128)} %constant.17.clone.1), kind=kCustom, calls=%fused_computation.5 | custom fusion | bytes 4194816 | tf_op jit(solution)/shard_map/scatter | solution.py:39
  55.6 4.8 %all-to-all-start.2 = ((f32[4,8,256,128]{3,2,1,0:T(8,128)}), f32[4,8,256,128]{3,2,1,0:T(8,128)}, u32[]{:S(2)}, u32[]{:S(2)}) async-start(f32[4,8,256,128]{3,2,1,0:T(8,128)} %bitcast.73), calls=%async_computation.3 | async-start | bytes 8388608 | tf_op jit(solution)/shard_map/all_to_all | solution.py:55
  61.1 46.2 %all-to-all-done.2 = f32[4,8,256,128]{3,2,1,0:T(8,128)} async-done(((f32[4,8,256,128]{3,2,1,0:T(8,128)}), f32[4,8,256,128]{3,2,1,0:T(8,128)}, u32[]{:S(2)}, u32[]{:S(2)}) %all-to-all-start.2) | async-done | bytes 4194336 | tf_op jit(solution)/shard_map/all_to_all | solution.py:55
  107.3 4.9 %all-to-all-start.1 = ((s32[4,8,256]{2,0,1:T(4,128)}), s32[4,8,256]{2,0,1:T(4,128)S(1)}, u32[]{:S(2)}, u32[]{:S(2)}) async-start(s32[4,8,256]{2,0,1:T(4,128)} %copy.38), calls=%async_computation.2 | async-start | bytes 65536 | tf_op jit(solution)/shard_map/all_to_all | solution.py:57
  112.2 1.9 fusion.12
  114.1 1.9 fusion.11
  116.0 1.9 fusion.10
  117.8 1.9 fusion.9
  119.7 1.9 fusion.8
  121.6 1.9 fusion.7
  123.5 1.9 fusion.6
  125.4 1.9 fusion.5
  127.3 5.2 %all-to-all-start.3 = ((f32[8,4,1,256,128]{4,3,1,2,0:T(8,128)}), f32[8,4,1,256,128]{4,3,1,2,0:T(8,128)}, u32[]{:S(2)}, u32[]{:S(2)}) async-start(f32[8,4,1,256,128]{4,3,1,2,0:T(8,128)} %fusion.5), calls=%async_computation.4 | async-start | bytes 8388608 | tf_op jit(solution)/shard_map/all_to_all | solution.py:12
  134.1 33.3 %reduce-scatter.2.cloned.1.call-done = f32[32,128]{1,0:T(8,128)} async-done(((f32[256,128]{1,0:T(8,128)}), f32[32,128]{1,0:T(8,128)}) %reduce-scatter.2.cloned.1.call-update) | async-done | bytes 16400 | tf_op jit(solution)/shard_map/reduce_scatter | solution.py:22
  167.4 15.7 %psum.7 = f32[32,128]{1,0:T(8,128)S(1)} all-reduce(f32[32,128]{1,0:T(8,128)} %reduce-scatter.2.cloned.1.call-done), channel_id=1, replica_groups=mesh['grp'=4,'dev'=8] {'grp'}, use_global_device_ids=true, to_apply=%region_1.2 | all-reduce | flops 4096 | bytes 32768 | tf_op jit(solution)/shard_map/psum | solution.py:23
  183.1 51.0 %all_gather.3 = f32[256,128]{1,0:T(8,128)S(1)} all-gather(f32[32,128]{1,0:T(8,128)S(1)} %psum.7), channel_id=1, replica_groups=mesh['grp'=4,'dev'=8] {'dev'}, dimensions={0}, use_global_device_ids=true | all-gather | bytes 147456 | tf_op jit(solution)/shard_map/all_gather | solution.py:24
  234.1 6.0 %scatter_custom_fusion = f32[8192,128]{1,0:T(8,128)} fusion(f32[8192,128]{1,0:T(8,128)} %copy.67, s32[256]{0:T(256)S(1)} %compare_select_fusion.2, f32[256,128]{1,0:T(8,128)S(1)} %all_gather.3, f32[]{:T(128)} %constant.14.clone.1), kind=kCustom, calls=%fused_computation.35 | custom fusion | flops 65536 | bytes 4325888 | tf_op jit(solution)/shard_map/scatter-add | solution.py:29
  240.1 2.6 multiply_bitcast_fusion
  242.6 2.2 copy.47
  244.8 57.0 %scatter_fusion = f32[8192,128]{1,0:T(8,128)} fusion(f32[8192,128]{1,0:T(8,128)} %scatter_custom_fusion, s32[8192]{0:T(1024)S(1)} %bitcast.77, f32[8192,128]{1,0:T(8,128)} %bitcast.72), kind=kCustom, calls=%fused_computation.3 | custom fusion | flops 1048576 | bytes 12615680 | tf_op jit(solution)/shard_map/scatter-add | solution.py:66
  (26 shorter events, 4.3 us)
Async XLA Ops:
  6.5 126.0 %copy-start = (f32[1024,128]{1,0:T(8,128)S(1)}, f32[1024,128]{1,0:T(8,128)}, u32[]{:S(2)}) copy-start(f32[1024,128]{1,0:T(8,128)} %param.11) | copy-start | bytes 1572868
  6.5 4.5 %copy-start.1 = (s32[4096,1]{0,1:T(1,128)S(1)}, s32[4096,1]{0,1:T(1,128)}, u32[]{:S(2)}) copy-start(s32[4096,1]{0,1:T(1,128)} %param.9) | copy-start | bytes 49156
  38.3 17.3 %all-to-all-start = ((s32[4,8,256]{2,1,0:T(8,128)}), s32[4,8,256]{2,1,0:T(8,128)S(1)}, u32[]{:S(2)}, u32[]{:S(2)}) async-start(s32[4,8,256]{2,1,0:T(8,128)} %reshape.61), calls=%async_computation.1 | async-start | bytes 65536 | tf_op jit(solution)/shard_map/all_to_all | solution.py:58
  55.6 51.7 %all-to-all-start.2 = ((f32[4,8,256,128]{3,2,1,0:T(8,128)}), f32[4,8,256,128]{3,2,1,0:T(8,128)}, u32[]{:S(2)}, u32[]{:S(2)}) async-start(f32[4,8,256,128]{3,2,1,0:T(8,128)} %bitcast.73), calls=%async_computation.3 | async-start | bytes 8388608 | tf_op jit(solution)/shard_map/all_to_all | solution.py:55
  107.3 19.9 %all-to-all-start.1 = ((s32[4,8,256]{2,0,1:T(4,128)}), s32[4,8,256]{2,0,1:T(4,128)S(1)}, u32[]{:S(2)}, u32[]{:S(2)}) async-start(s32[4,8,256]{2,0,1:T(4,128)} %copy.38), calls=%async_computation.2 | async-start | bytes 65536 | tf_op jit(solution)/shard_map/all_to_all | solution.py:57
  127.3 5.3 %copy-start.2 = (s32[1024]{0:T(1024)S(1)}, s32[1024]{0:T(1024)}, u32[]{:S(2)}) copy-start(s32[1024]{0:T(1024)} %param.12) | copy-start | bytes 12292
  127.3 6.7 %copy-start.3 = (s32[256]{0:T(256)S(1)}, s32[256]{0:T(256)}, u32[]{:S(2)}) copy-start(s32[256]{0:T(256)} %param.13) | copy-start | bytes 3076
  127.3 112.8 %all-to-all-start.3 = ((f32[8,4,1,256,128]{4,3,1,2,0:T(8,128)}), f32[8,4,1,256,128]{4,3,1,2,0:T(8,128)}, u32[]{:S(2)}, u32[]{:S(2)}) async-start(f32[8,4,1,256,128]{4,3,1,2,0:T(8,128)} %fusion.5), calls=%async_computation.4 | async-start | bytes 8388608 | tf_op jit(solution)/shard_map/all_to_all | solution.py:12
  132.5 34.9 %reduce-scatter.2.cloned.1.call-start = ((), (), s32[]{:S(2)}) async-start(), calls=%async_computation.5 | async-start | bytes 147456 | tf_op jit(solution)/shard_map/reduce_scatter | solution.py:22
Sparse Core Ops, SparseCore 0:
  135.5 31.7 reduce-scatter.1
